TPU v7x, 32 devices: a whole 2x2x4 slice. The times are simulated.
32 devices in a mesh: pb: 4 (over x, core), kv: 8 (over z, y).
Axes of the slice: x: 2, y: 2, z: 4, core: 2. Of those that a mesh axis runs over, the one named last changes fastest.
Arguments:
- queries: bfloat16 [32768, 256], P(('pb', 'kv')), may hold values from -64 to 64
- keys: bfloat16 [1024, 256], P('kv'), may hold values from -6 to 6
- values: bfloat16 [1024, 256], P('kv'), may hold values from -6 to 6
- dout: bfloat16 [32768, 256], P(('pb', 'kv')), may hold values from -256 to 256
Outputs:
- dq: float32 [32768, 256], P(('pb', 'kv'))
- dk: float32 [1024, 256], P('kv')
- dv: float32 [1024, 256], P('kv')
All inputs are finite; a program needn't handle non-finite values.
Results may differ from a plain program's by a relative error of at most 0.0029.
Values may be sent and summed in bfloat16 or wider, within the bound.
No kernel may reach another device: no remote copies, remote signals or barrier semaphores. Data moves between devices by JAX's collectives and lax.ppermute only.
A program may use at most 64 MiB of HBM per device.

v0:
```python
import math
import jax
import jax.numpy as jnp
from jax import lax
from jax.sharding import PartitionSpec as P

H = 2
DH = 128


def from_behind(value, axis, by):
    peers = lax.axis_size(axis)
    return lax.ppermute(value, axis, [(i, (i + by) % peers) for i in range(peers)])


def split_heads(matrix):
    return matrix.reshape(matrix.shape[0], H, DH)


def block_scores(query_blk, grad_blk, key_blk, value_blk):
    score_scale = 1.0 / math.sqrt(DH)
    logits = (
        jnp.einsum("qhd,khd->hqk", query_blk, key_blk, preferred_element_type=jnp.float32)
        * score_scale
    )
    dprob = jnp.einsum("qhd,khd->hqk", grad_blk, value_blk, preferred_element_type=jnp.float32)
    return (logits, dprob)


def empty_stats(row_count):
    return (
        jnp.full((H, row_count), -1e30, jnp.float32),
        jnp.zeros((H, row_count), jnp.float32),
        jnp.zeros((H, row_count), jnp.float32),
    )


def fold_stats(totals, logits, dprob):
    peak, mass, weighted = totals
    new_peak = jnp.maximum(peak, jnp.max(logits, axis=-1))
    keep = jnp.exp(peak - new_peak)
    shifted = jnp.exp(logits - new_peak[..., None])
    return (
        new_peak,
        mass * keep + jnp.sum(shifted, axis=-1),
        weighted * keep + jnp.sum(shifted * dprob, axis=-1),
    )


def block_grads(query_blk, grad_blk, key_blk, value_blk, lse, delta):
    score_scale = 1.0 / math.sqrt(DH)
    logits, dprob = block_scores(query_blk, grad_blk, key_blk, value_blk)
    probs = jnp.exp(logits - lse[..., None])
    dlogits = probs * (dprob - delta[..., None])
    probs_b = probs.astype(jnp.bfloat16)
    dlogits_b = dlogits.astype(jnp.bfloat16)
    dv_part = jnp.einsum("hqk,qhd->khd", probs_b, grad_blk, preferred_element_type=jnp.float32)
    dk_part = (
        jnp.einsum("hqk,qhd->khd", dlogits_b, query_blk, preferred_element_type=jnp.float32)
        * score_scale
    )
    dq_part = (
        jnp.einsum("hqk,khd->qhd", dlogits_b, key_blk, preferred_element_type=jnp.float32)
        * score_scale
    )
    return (dq_part, dk_part, dv_part)


def local(queries, keys, values, dout):
    cycle_size = lax.axis_size("kv")
    query_rows = queries.shape[0]
    key_rows = keys.shape[0]
    query_heads = split_heads(queries)
    grad_heads = split_heads(dout)
    key_vals = jnp.stack([split_heads(keys), split_heads(values)])

    def stat_step(step_index, carry):
        moving, totals = carry
        logits, dprob = block_scores(query_heads, grad_heads, moving[0], moving[1])
        totals = fold_stats(totals, logits, dprob)
        moving = from_behind(moving, "kv", 1)
        return (moving, totals)

    key_vals, totals = lax.fori_loop(0, cycle_size, stat_step, (key_vals, empty_stats(query_rows)))
    lse = totals[0] + jnp.log(totals[1])
    delta = totals[2] / totals[1]

    def grad_step(step_index, carry):
        moving, grads_acc, dq_acc = carry
        dq_part, dk_part, dv_part = block_grads(
            query_heads, grad_heads, moving[0], moving[1], lse, delta
        )
        grads_acc = grads_acc + jnp.stack([dk_part, dv_part])
        moving = from_behind(moving, "kv", 1)
        grads_acc = from_behind(grads_acc, "kv", 1)
        return (moving, grads_acc, dq_acc + dq_part)

    start = (
        key_vals,
        jnp.zeros((2, key_rows, H, DH), jnp.float32),
        jnp.zeros((query_rows, H, DH), jnp.float32),
    )
    key_vals, grads_acc, dq_acc = lax.fori_loop(0, cycle_size, grad_step, start)
    dq = dq_acc.reshape(query_rows, H * DH)
    summed = lax.psum(grads_acc, "pb")
    return (dq, summed[0].reshape(key_rows, H * DH), summed[1].reshape(key_rows, H * DH))


def solution(mesh):
    return jax.shard_map(
        local,
        mesh=mesh,
        in_specs=(P(("pb", "kv"), None), P("kv", None), P("kv", None), P(("pb", "kv"), None)),
        out_specs=(P(("pb", "kv"), None), P("kv", None), P("kv", None)),
        check_vma=False,
    )
```

profile of v0, /device:TPU:0, one launch (start us, length us, event | category | flops | bytes accessed | tf_op | source)
XLA Modules:
  0.0 225.6 jit_solution(1667497110011160057)
XLA Ops:
  7.2 1.2 copy.16
  8.8 0.8 copy-done.1
  10.0 0.6 copy-done.2
  10.7 0.7 copy-done.3
  11.7 66.0 %while.32 = (s32[]{:T(128)}, bf16[2,128,2,128]{3,1,2,0:T(8,128)(2,1)S(1)}, f32[2,1024]{1,0:T(2,128)S(1)}, f32[2,1024]{1,0:T(2,128)S(1)}, f32[2,1024]{1,0:T(2,128...) while((s32[]{:T(128)}, ...), condition=%wide.region_4.0_spmd.clone, body=%wide.region_0.0_spmd.clone.sunk | while | flops 136067072 | bytes 5259408 | solution.py:84
  11.7 3.0 %collective-permute-start = (bf16[2,128,2,128]{3,1,2,0:T(8,128)(2,1)S(1)}, bf16[2,128,2,128]{3,1,2,0:T(8,128)(2,1)S(1)}, u32[]{:S(2)}, u32[]{:S(2)}) collective-permute-start(bf16[2,128,2,128]{3,1,2,0:T(8,128)(2,1)S(1)} %copy.40), channel_id=1, source_target_pairs={{0,1},{1,2},{2,3},{3,4},{4,5},{5,6},{6,7},{7,0},{8,9},{9,10},{10,1... | collective-permute-start | bytes 393224 | tf_op jit(solution)/shard_map/while/body/eval_jaxpr/ppermute | solution.py:13
  15.7 5.7 %collective-permute-done = bf16[2,128,2,128]{3,1,2,0:T(8,128)(2,1)S(1)} collective-permute-done((bf16[2,128,2,128]{3,1,2,0:T(8,128)(2,1)S(1)}, bf16[2,128,2,128]{3,1,2,0:T(8,128)(2,1)S(1)}, u32[]{:S(2)}, u32[]{:S(2)}) %collective-permute-start) | collective-permute-done | bytes 131104 | tf_op jit(solution)/shard_map/while/body/eval_jaxpr/ppermute | solution.py:13
  22.3 6.8 %collective-permute-done = bf16[2,128,2,128]{3,1,2,0:T(8,128)(2,1)S(1)} collective-permute-done((bf16[2,128,2,128]{3,1,2,0:T(8,128)(2,1)S(1)}, bf16[2,128,2,128]{3,1,2,0:T(8,128)(2,1)S(1)}, u32[]{:S(2)}, u32[]{:S(2)}) %collective-permute-start) | collective-permute-done | bytes 131104 | tf_op jit(solution)/shard_map/while/body/eval_jaxpr/ppermute | solution.py:13
  30.0 6.8 %collective-permute-done = bf16[2,128,2,128]{3,1,2,0:T(8,128)(2,1)S(1)} collective-permute-done((bf16[2,128,2,128]{3,1,2,0:T(8,128)(2,1)S(1)}, bf16[2,128,2,128]{3,1,2,0:T(8,128)(2,1)S(1)}, u32[]{:S(2)}, u32[]{:S(2)}) %collective-permute-start) | collective-permute-done | bytes 131104 | tf_op jit(solution)/shard_map/while/body/eval_jaxpr/ppermute | solution.py:13
  37.8 6.8 %collective-permute-done = bf16[2,128,2,128]{3,1,2,0:T(8,128)(2,1)S(1)} collective-permute-done((bf16[2,128,2,128]{3,1,2,0:T(8,128)(2,1)S(1)}, bf16[2,128,2,128]{3,1,2,0:T(8,128)(2,1)S(1)}, u32[]{:S(2)}, u32[]{:S(2)}) %collective-permute-start) | collective-permute-done | bytes 131104 | tf_op jit(solution)/shard_map/while/body/eval_jaxpr/ppermute | solution.py:13
  45.5 6.8 %collective-permute-done = bf16[2,128,2,128]{3,1,2,0:T(8,128)(2,1)S(1)} collective-permute-done((bf16[2,128,2,128]{3,1,2,0:T(8,128)(2,1)S(1)}, bf16[2,128,2,128]{3,1,2,0:T(8,128)(2,1)S(1)}, u32[]{:S(2)}, u32[]{:S(2)}) %collective-permute-start) | collective-permute-done | bytes 131104 | tf_op jit(solution)/shard_map/while/body/eval_jaxpr/ppermute | solution.py:13
  53.2 7.9 %collective-permute-done = bf16[2,128,2,128]{3,1,2,0:T(8,128)(2,1)S(1)} collective-permute-done((bf16[2,128,2,128]{3,1,2,0:T(8,128)(2,1)S(1)}, bf16[2,128,2,128]{3,1,2,0:T(8,128)(2,1)S(1)}, u32[]{:S(2)}, u32[]{:S(2)}) %collective-permute-start) | collective-permute-done | bytes 131104 | tf_op jit(solution)/shard_map/while/body/eval_jaxpr/ppermute | solution.py:13
  62.1 7.3 %collective-permute-done = bf16[2,128,2,128]{3,1,2,0:T(8,128)(2,1)S(1)} collective-permute-done((bf16[2,128,2,128]{3,1,2,0:T(8,128)(2,1)S(1)}, bf16[2,128,2,128]{3,1,2,0:T(8,128)(2,1)S(1)}, u32[]{:S(2)}, u32[]{:S(2)}) %collective-permute-start) | collective-permute-done | bytes 131104 | tf_op jit(solution)/shard_map/while/body/eval_jaxpr/ppermute | solution.py:13
  70.4 7.4 %collective-permute-done = bf16[2,128,2,128]{3,1,2,0:T(8,128)(2,1)S(1)} collective-permute-done((bf16[2,128,2,128]{3,1,2,0:T(8,128)(2,1)S(1)}, bf16[2,128,2,128]{3,1,2,0:T(8,128)(2,1)S(1)}, u32[]{:S(2)}, u32[]{:S(2)}) %collective-permute-start) | collective-permute-done | bytes 131104 | tf_op jit(solution)/shard_map/while/body/eval_jaxpr/ppermute | solution.py:13
  77.8 106.9 %while.33 = (s32[]{:T(128)}, bf16[2,128,2,128]{3,1,2,0:T(8,128)(2,1)S(1)}, f32[2,128,2,128]{3,1,2,0:T(8,128)S(1)}, f32[1024,2,128]{2,0,1:T(8,128)S(1)}, bf16[102...) while((s32[]{:T(128)}, ...), condition=%wide.region_6.0_spmd.clone, body=%wide.region_5.0_spmd.clone.sunk | while | flops 338067456 | bytes 12009663 | solution.py:103
  79.4 0.7 maximum_add_fusion.2
  80.1 0.4 fusion.78
  80.5 5.5 %collective-permute-done.1 = bf16[2,128,2,128]{3,1,2,0:T(8,128)(2,1)S(1)} collective-permute-done((bf16[2,128,2,128]{3,1,2,0:T(8,128)(2,1)S(1)}, bf16[2,128,2,128]{3,1,2,0:T(8,128)(2,1)S(1)}, u32[]{:S(2)}, u32[]{:S(2)}) %collective-permute-start.1) | collective-permute-done | bytes 131104 | tf_op jit(solution)/shard_map/while/body/eval_jaxpr/ppermute | solution.py:13
  86.0 6.0 %collective-permute-done.2 = f32[2,128,2,128]{3,1,2,0:T(8,128)S(1)} collective-permute-done((f32[2,128,2,128]{3,1,2,0:T(8,128)}, f32[2,128,2,128]{3,1,2,0:T(8,128)S(1)}, u32[]{:S(2)}, u32[]{:S(2)}) %collective-permute-start.2) | collective-permute-done | bytes 262176 | tf_op jit(solution)/shard_map/while/body/eval_jaxpr/ppermute | solution.py:13
  93.5 0.7 maximum_add_fusion.2
  94.7 6.2 %collective-permute-done.1 = bf16[2,128,2,128]{3,1,2,0:T(8,128)(2,1)S(1)} collective-permute-done((bf16[2,128,2,128]{3,1,2,0:T(8,128)(2,1)S(1)}, bf16[2,128,2,128]{3,1,2,0:T(8,128)(2,1)S(1)}, u32[]{:S(2)}, u32[]{:S(2)}) %collective-permute-start.1) | collective-permute-done | bytes 131104 | tf_op jit(solution)/shard_map/while/body/eval_jaxpr/ppermute | solution.py:13
  100.9 5.2 %collective-permute-done.2 = f32[2,128,2,128]{3,1,2,0:T(8,128)S(1)} collective-permute-done((f32[2,128,2,128]{3,1,2,0:T(8,128)}, f32[2,128,2,128]{3,1,2,0:T(8,128)S(1)}, u32[]{:S(2)}, u32[]{:S(2)}) %collective-permute-start.2) | collective-permute-done | bytes 262176 | tf_op jit(solution)/shard_map/while/body/eval_jaxpr/ppermute | solution.py:13
  107.7 0.7 maximum_add_fusion.2
  108.9 5.6 %collective-permute-done.1 = bf16[2,128,2,128]{3,1,2,0:T(8,128)(2,1)S(1)} collective-permute-done((bf16[2,128,2,128]{3,1,2,0:T(8,128)(2,1)S(1)}, bf16[2,128,2,128]{3,1,2,0:T(8,128)(2,1)S(1)}, u32[]{:S(2)}, u32[]{:S(2)}) %collective-permute-start.1) | collective-permute-done | bytes 131104 | tf_op jit(solution)/shard_map/while/body/eval_jaxpr/ppermute | solution.py:13
  114.4 5.2 %collective-permute-done.2 = f32[2,128,2,128]{3,1,2,0:T(8,128)S(1)} collective-permute-done((f32[2,128,2,128]{3,1,2,0:T(8,128)}, f32[2,128,2,128]{3,1,2,0:T(8,128)S(1)}, u32[]{:S(2)}, u32[]{:S(2)}) %collective-permute-start.2) | collective-permute-done | bytes 262176 | tf_op jit(solution)/shard_map/while/body/eval_jaxpr/ppermute | solution.py:13
  121.2 0.7 maximum_add_fusion.2
  122.0 0.4 fusion.78
  122.4 5.7 %collective-permute-done.1 = bf16[2,128,2,128]{3,1,2,0:T(8,128)(2,1)S(1)} collective-permute-done((bf16[2,128,2,128]{3,1,2,0:T(8,128)(2,1)S(1)}, bf16[2,128,2,128]{3,1,2,0:T(8,128)(2,1)S(1)}, u32[]{:S(2)}, u32[]{:S(2)}) %collective-permute-start.1) | collective-permute-done | bytes 131104 | tf_op jit(solution)/shard_map/while/body/eval_jaxpr/ppermute | solution.py:13
  128.1 4.9 %collective-permute-done.2 = f32[2,128,2,128]{3,1,2,0:T(8,128)S(1)} collective-permute-done((f32[2,128,2,128]{3,1,2,0:T(8,128)}, f32[2,128,2,128]{3,1,2,0:T(8,128)S(1)}, u32[]{:S(2)}, u32[]{:S(2)}) %collective-permute-start.2) | collective-permute-done | bytes 262176 | tf_op jit(solution)/shard_map/while/body/eval_jaxpr/ppermute | solution.py:13
  134.6 0.7 maximum_add_fusion.2
  135.3 0.4 fusion.78
  135.7 5.9 %collective-permute-done.1 = bf16[2,128,2,128]{3,1,2,0:T(8,128)(2,1)S(1)} collective-permute-done((bf16[2,128,2,128]{3,1,2,0:T(8,128)(2,1)S(1)}, bf16[2,128,2,128]{3,1,2,0:T(8,128)(2,1)S(1)}, u32[]{:S(2)}, u32[]{:S(2)}) %collective-permute-start.1) | collective-permute-done | bytes 131104 | tf_op jit(solution)/shard_map/while/body/eval_jaxpr/ppermute | solution.py:13
  141.6 4.8 %collective-permute-done.2 = f32[2,128,2,128]{3,1,2,0:T(8,128)S(1)} collective-permute-done((f32[2,128,2,128]{3,1,2,0:T(8,128)}, f32[2,128,2,128]{3,1,2,0:T(8,128)S(1)}, u32[]{:S(2)}, u32[]{:S(2)}) %collective-permute-start.2) | collective-permute-done | bytes 262176 | tf_op jit(solution)/shard_map/while/body/eval_jaxpr/ppermute | solution.py:13
  147.9 0.7 maximum_add_fusion.2
  149.1 5.9 %collective-permute-done.1 = bf16[2,128,2,128]{3,1,2,0:T(8,128)(2,1)S(1)} collective-permute-done((bf16[2,128,2,128]{3,1,2,0:T(8,128)(2,1)S(1)}, bf16[2,128,2,128]{3,1,2,0:T(8,128)(2,1)S(1)}, u32[]{:S(2)}, u32[]{:S(2)}) %collective-permute-start.1) | collective-permute-done | bytes 131104 | tf_op jit(solution)/shard_map/while/body/eval_jaxpr/ppermute | solution.py:13
  155.0 4.8 %collective-permute-done.2 = f32[2,128,2,128]{3,1,2,0:T(8,128)S(1)} collective-permute-done((f32[2,128,2,128]{3,1,2,0:T(8,128)}, f32[2,128,2,128]{3,1,2,0:T(8,128)S(1)}, u32[]{:S(2)}, u32[]{:S(2)}) %collective-permute-start.2) | collective-permute-done | bytes 262176 | tf_op jit(solution)/shard_map/while/body/eval_jaxpr/ppermute | solution.py:13
  161.3 0.7 maximum_add_fusion.2
  162.0 0.4 fusion.78
  162.4 5.9 %collective-permute-done.1 = bf16[2,128,2,128]{3,1,2,0:T(8,128)(2,1)S(1)} collective-permute-done((bf16[2,128,2,128]{3,1,2,0:T(8,128)(2,1)S(1)}, bf16[2,128,2,128]{3,1,2,0:T(8,128)(2,1)S(1)}, u32[]{:S(2)}, u32[]{:S(2)}) %collective-permute-start.1) | collective-permute-done | bytes 131104 | tf_op jit(solution)/shard_map/while/body/eval_jaxpr/ppermute | solution.py:13
  168.3 4.8 %collective-permute-done.2 = f32[2,128,2,128]{3,1,2,0:T(8,128)S(1)} collective-permute-done((f32[2,128,2,128]{3,1,2,0:T(8,128)}, f32[2,128,2,128]{3,1,2,0:T(8,128)S(1)}, u32[]{:S(2)}, u32[]{:S(2)}) %collective-permute-start.2) | collective-permute-done | bytes 262176 | tf_op jit(solution)/shard_map/while/body/eval_jaxpr/ppermute | solution.py:13
  174.6 0.7 maximum_add_fusion.2
  175.8 5.0 %collective-permute-done.1 = bf16[2,128,2,128]{3,1,2,0:T(8,128)(2,1)S(1)} collective-permute-done((bf16[2,128,2,128]{3,1,2,0:T(8,128)(2,1)S(1)}, bf16[2,128,2,128]{3,1,2,0:T(8,128)(2,1)S(1)}, u32[]{:S(2)}, u32[]{:S(2)}) %collective-permute-start.1) | collective-permute-done | bytes 131104 | tf_op jit(solution)/shard_map/while/body/eval_jaxpr/ppermute | solution.py:13
  180.8 3.8 %collective-permute-done.2 = f32[2,128,2,128]{3,1,2,0:T(8,128)S(1)} collective-permute-done((f32[2,128,2,128]{3,1,2,0:T(8,128)}, f32[2,128,2,128]{3,1,2,0:T(8,128)S(1)}, u32[]{:S(2)}, u32[]{:S(2)}) %collective-permute-start.2) | collective-permute-done | bytes 262176 | tf_op jit(solution)/shard_map/while/body/eval_jaxpr/ppermute | solution.py:13
  184.7 0.7 copy-done
  185.4 1.1 copy_bitcast_fusion
  186.4 30.3 %all-reduce.2.cloned.1.call-done = f32[2,128,2,128]{3,1,2,0:T(8,128)} async-done(((f32[2,128,2,128]{3,1,2,0:T(8,128)}), f32[2,128,2,128]{3,1,2,0:T(8,128)}) %all-reduce.2.cloned.1.call-update) | async-done | bytes 262160 | tf_op jit(solution)/shard_map/psum | solution.py:105
  216.8 1.0 fusion.24
  218.0 0.7 copy_bitcast_fusion.1
  (144 shorter events, 22.5 us)
Async XLA Ops:
  7.2 209.6 %all-reduce.2.cloned.1.call-start = ((), (), s32[]{:S(2)}) async-start(), calls=%async_computation | async-start | bytes 524288 | tf_op jit(solution)/shard_map/psum | solution.py:105
  8.5 1.0 copy-start.1
  9.8 0.8 copy-start.2
  10.6 0.8 copy-start.3
  11.7 9.6 %collective-permute-start = (bf16[2,128,2,128]{3,1,2,0:T(8,128)(2,1)S(1)}, bf16[2,128,2,128]{3,1,2,0:T(8,128)(2,1)S(1)}, u32[]{:S(2)}, u32[]{:S(2)}) collective-permute-start(bf16[2,128,2,128]{3,1,2,0:T(8,128)(2,1)S(1)} %copy.40), channel_id=1, source_target_pairs={{0,1},{1,2},{2,3},{3,4},{4,5},{5,6},{6,7},{7,0},{8,9},{9,10},{10,1... | collective-permute-start | bytes 393224 | tf_op jit(solution)/shard_map/while/body/eval_jaxpr/ppermute | solution.py:13
  21.3 7.7 %collective-permute-start = (bf16[2,128,2,128]{3,1,2,0:T(8,128)(2,1)S(1)}, bf16[2,128,2,128]{3,1,2,0:T(8,128)(2,1)S(1)}, u32[]{:S(2)}, u32[]{:S(2)}) collective-permute-start(bf16[2,128,2,128]{3,1,2,0:T(8,128)(2,1)S(1)} %copy.40), channel_id=1, source_target_pairs={{0,1},{1,2},{2,3},{3,4},{4,5},{5,6},{6,7},{7,0},{8,9},{9,10},{10,1... | collective-permute-start | bytes 393224 | tf_op jit(solution)/shard_map/while/body/eval_jaxpr/ppermute | solution.py:13
  29.1 7.7 %collective-permute-start = (bf16[2,128,2,128]{3,1,2,0:T(8,128)(2,1)S(1)}, bf16[2,128,2,128]{3,1,2,0:T(8,128)(2,1)S(1)}, u32[]{:S(2)}, u32[]{:S(2)}) collective-permute-start(bf16[2,128,2,128]{3,1,2,0:T(8,128)(2,1)S(1)} %copy.40), channel_id=1, source_target_pairs={{0,1},{1,2},{2,3},{3,4},{4,5},{5,6},{6,7},{7,0},{8,9},{9,10},{10,1... | collective-permute-start | bytes 393224 | tf_op jit(solution)/shard_map/while/body/eval_jaxpr/ppermute | solution.py:13
  36.8 7.7 %collective-permute-start = (bf16[2,128,2,128]{3,1,2,0:T(8,128)(2,1)S(1)}, bf16[2,128,2,128]{3,1,2,0:T(8,128)(2,1)S(1)}, u32[]{:S(2)}, u32[]{:S(2)}) collective-permute-start(bf16[2,128,2,128]{3,1,2,0:T(8,128)(2,1)S(1)} %copy.40), channel_id=1, source_target_pairs={{0,1},{1,2},{2,3},{3,4},{4,5},{5,6},{6,7},{7,0},{8,9},{9,10},{10,1... | collective-permute-start | bytes 393224 | tf_op jit(solution)/shard_map/while/body/eval_jaxpr/ppermute | solution.py:13
  44.5 7.7 %collective-permute-start = (bf16[2,128,2,128]{3,1,2,0:T(8,128)(2,1)S(1)}, bf16[2,128,2,128]{3,1,2,0:T(8,128)(2,1)S(1)}, u32[]{:S(2)}, u32[]{:S(2)}) collective-permute-start(bf16[2,128,2,128]{3,1,2,0:T(8,128)(2,1)S(1)} %copy.40), channel_id=1, source_target_pairs={{0,1},{1,2},{2,3},{3,4},{4,5},{5,6},{6,7},{7,0},{8,9},{9,10},{10,1... | collective-permute-start | bytes 393224 | tf_op jit(solution)/shard_map/while/body/eval_jaxpr/ppermute | solution.py:13
  52.3 8.8 %collective-permute-start = (bf16[2,128,2,128]{3,1,2,0:T(8,128)(2,1)S(1)}, bf16[2,128,2,128]{3,1,2,0:T(8,128)(2,1)S(1)}, u32[]{:S(2)}, u32[]{:S(2)}) collective-permute-start(bf16[2,128,2,128]{3,1,2,0:T(8,128)(2,1)S(1)} %copy.40), channel_id=1, source_target_pairs={{0,1},{1,2},{2,3},{3,4},{4,5},{5,6},{6,7},{7,0},{8,9},{9,10},{10,1... | collective-permute-start | bytes 393224 | tf_op jit(solution)/shard_map/while/body/eval_jaxpr/ppermute | solution.py:13
  61.1 8.3 %collective-permute-start = (bf16[2,128,2,128]{3,1,2,0:T(8,128)(2,1)S(1)}, bf16[2,128,2,128]{3,1,2,0:T(8,128)(2,1)S(1)}, u32[]{:S(2)}, u32[]{:S(2)}) collective-permute-start(bf16[2,128,2,128]{3,1,2,0:T(8,128)(2,1)S(1)} %copy.40), channel_id=1, source_target_pairs={{0,1},{1,2},{2,3},{3,4},{4,5},{5,6},{6,7},{7,0},{8,9},{9,10},{10,1... | collective-permute-start | bytes 393224 | tf_op jit(solution)/shard_map/while/body/eval_jaxpr/ppermute | solution.py:13
  69.4 8.3 %collective-permute-start = (bf16[2,128,2,128]{3,1,2,0:T(8,128)(2,1)S(1)}, bf16[2,128,2,128]{3,1,2,0:T(8,128)(2,1)S(1)}, u32[]{:S(2)}, u32[]{:S(2)}) collective-permute-start(bf16[2,128,2,128]{3,1,2,0:T(8,128)(2,1)S(1)} %copy.40), channel_id=1, source_target_pairs={{0,1},{1,2},{2,3},{3,4},{4,5},{5,6},{6,7},{7,0},{8,9},{9,10},{10,1... | collective-permute-start | bytes 393224 | tf_op jit(solution)/shard_map/while/body/eval_jaxpr/ppermute | solution.py:13
  77.8 8.1 %collective-permute-start.1 = (bf16[2,128,2,128]{3,1,2,0:T(8,128)(2,1)S(1)}, bf16[2,128,2,128]{3,1,2,0:T(8,128)(2,1)S(1)}, u32[]{:S(2)}, u32[]{:S(2)}) collective-permute-start(bf16[2,128,2,128]{3,1,2,0:T(8,128)(2,1)S(1)} %copy.54), channel_id=1, source_target_pairs={{0,1},{1,2},{2,3},{3,4},{4,5},{5,6},{6,7},{7,0},{8,9},{9,10},{10,1... | collective-permute-start | bytes 393224 | tf_op jit(solution)/shard_map/while/body/eval_jaxpr/ppermute | solution.py:13
  80.1 11.9 %collective-permute-start.2 = (f32[2,128,2,128]{3,1,2,0:T(8,128)}, f32[2,128,2,128]{3,1,2,0:T(8,128)S(1)}, u32[]{:S(2)}, u32[]{:S(2)}) collective-permute-start(f32[2,128,2,128]{3,1,2,0:T(8,128)} %maximum_add_fusion.2), channel_id=1, source_target_pairs={{0,1},{1,2},{2,3},{3,4},{4,5},{5,6},{6,7},{7,0},{8,9},{9,10},{10,1... | collective-permute-start | bytes 786440 | tf_op jit(solution)/shard_map/while/body/eval_jaxpr/ppermute | solution.py:13
  92.0 8.9 %collective-permute-start.1 = (bf16[2,128,2,128]{3,1,2,0:T(8,128)(2,1)S(1)}, bf16[2,128,2,128]{3,1,2,0:T(8,128)(2,1)S(1)}, u32[]{:S(2)}, u32[]{:S(2)}) collective-permute-start(bf16[2,128,2,128]{3,1,2,0:T(8,128)(2,1)S(1)} %copy.54), channel_id=1, source_target_pairs={{0,1},{1,2},{2,3},{3,4},{4,5},{5,6},{6,7},{7,0},{8,9},{9,10},{10,1... | collective-permute-start | bytes 393224 | tf_op jit(solution)/shard_map/while/body/eval_jaxpr/ppermute | solution.py:13
  94.3 11.9 %collective-permute-start.2 = (f32[2,128,2,128]{3,1,2,0:T(8,128)}, f32[2,128,2,128]{3,1,2,0:T(8,128)S(1)}, u32[]{:S(2)}, u32[]{:S(2)}) collective-permute-start(f32[2,128,2,128]{3,1,2,0:T(8,128)} %maximum_add_fusion.2), channel_id=1, source_target_pairs={{0,1},{1,2},{2,3},{3,4},{4,5},{5,6},{6,7},{7,0},{8,9},{9,10},{10,1... | collective-permute-start | bytes 786440 | tf_op jit(solution)/shard_map/while/body/eval_jaxpr/ppermute | solution.py:13
  106.2 8.3 %collective-permute-start.1 = (bf16[2,128,2,128]{3,1,2,0:T(8,128)(2,1)S(1)}, bf16[2,128,2,128]{3,1,2,0:T(8,128)(2,1)S(1)}, u32[]{:S(2)}, u32[]{:S(2)}) collective-permute-start(bf16[2,128,2,128]{3,1,2,0:T(8,128)(2,1)S(1)} %copy.54), channel_id=1, source_target_pairs={{0,1},{1,2},{2,3},{3,4},{4,5},{5,6},{6,7},{7,0},{8,9},{9,10},{10,1... | collective-permute-start | bytes 393224 | tf_op jit(solution)/shard_map/while/body/eval_jaxpr/ppermute | solution.py:13
  108.5 11.2 %collective-permute-start.2 = (f32[2,128,2,128]{3,1,2,0:T(8,128)}, f32[2,128,2,128]{3,1,2,0:T(8,128)S(1)}, u32[]{:S(2)}, u32[]{:S(2)}) collective-permute-start(f32[2,128,2,128]{3,1,2,0:T(8,128)} %maximum_add_fusion.2), channel_id=1, source_target_pairs={{0,1},{1,2},{2,3},{3,4},{4,5},{5,6},{6,7},{7,0},{8,9},{9,10},{10,1... | collective-permute-start | bytes 786440 | tf_op jit(solution)/shard_map/while/body/eval_jaxpr/ppermute | solution.py:13
  119.7 8.4 %collective-permute-start.1 = (bf16[2,128,2,128]{3,1,2,0:T(8,128)(2,1)S(1)}, bf16[2,128,2,128]{3,1,2,0:T(8,128)(2,1)S(1)}, u32[]{:S(2)}, u32[]{:S(2)}) collective-permute-start(bf16[2,128,2,128]{3,1,2,0:T(8,128)(2,1)S(1)} %copy.54), channel_id=1, source_target_pairs={{0,1},{1,2},{2,3},{3,4},{4,5},{5,6},{6,7},{7,0},{8,9},{9,10},{10,1... | collective-permute-start | bytes 393224 | tf_op jit(solution)/shard_map/while/body/eval_jaxpr/ppermute | solution.py:13
  122.0 11.1 %collective-permute-start.2 = (f32[2,128,2,128]{3,1,2,0:T(8,128)}, f32[2,128,2,128]{3,1,2,0:T(8,128)S(1)}, u32[]{:S(2)}, u32[]{:S(2)}) collective-permute-start(f32[2,128,2,128]{3,1,2,0:T(8,128)} %maximum_add_fusion.2), channel_id=1, source_target_pairs={{0,1},{1,2},{2,3},{3,4},{4,5},{5,6},{6,7},{7,0},{8,9},{9,10},{10,1... | collective-permute-start | bytes 786440 | tf_op jit(solution)/shard_map/while/body/eval_jaxpr/ppermute | solution.py:13
  133.1 8.6 %collective-permute-start.1 = (bf16[2,128,2,128]{3,1,2,0:T(8,128)(2,1)S(1)}, bf16[2,128,2,128]{3,1,2,0:T(8,128)(2,1)S(1)}, u32[]{:S(2)}, u32[]{:S(2)}) collective-permute-start(bf16[2,128,2,128]{3,1,2,0:T(8,128)(2,1)S(1)} %copy.54), channel_id=1, source_target_pairs={{0,1},{1,2},{2,3},{3,4},{4,5},{5,6},{6,7},{7,0},{8,9},{9,10},{10,1... | collective-permute-start | bytes 393224 | tf_op jit(solution)/shard_map/while/body/eval_jaxpr/ppermute | solution.py:13
  135.3 11.1 %collective-permute-start.2 = (f32[2,128,2,128]{3,1,2,0:T(8,128)}, f32[2,128,2,128]{3,1,2,0:T(8,128)S(1)}, u32[]{:S(2)}, u32[]{:S(2)}) collective-permute-start(f32[2,128,2,128]{3,1,2,0:T(8,128)} %maximum_add_fusion.2), channel_id=1, source_target_pairs={{0,1},{1,2},{2,3},{3,4},{4,5},{5,6},{6,7},{7,0},{8,9},{9,10},{10,1... | collective-permute-start | bytes 786440 | tf_op jit(solution)/shard_map/while/body/eval_jaxpr/ppermute | solution.py:13
  146.4 8.6 %collective-permute-start.1 = (bf16[2,128,2,128]{3,1,2,0:T(8,128)(2,1)S(1)}, bf16[2,128,2,128]{3,1,2,0:T(8,128)(2,1)S(1)}, u32[]{:S(2)}, u32[]{:S(2)}) collective-permute-start(bf16[2,128,2,128]{3,1,2,0:T(8,128)(2,1)S(1)} %copy.54), channel_id=1, source_target_pairs={{0,1},{1,2},{2,3},{3,4},{4,5},{5,6},{6,7},{7,0},{8,9},{9,10},{10,1... | collective-permute-start | bytes 393224 | tf_op jit(solution)/shard_map/while/body/eval_jaxpr/ppermute | solution.py:13
  148.7 11.1 %collective-permute-start.2 = (f32[2,128,2,128]{3,1,2,0:T(8,128)}, f32[2,128,2,128]{3,1,2,0:T(8,128)S(1)}, u32[]{:S(2)}, u32[]{:S(2)}) collective-permute-start(f32[2,128,2,128]{3,1,2,0:T(8,128)} %maximum_add_fusion.2), channel_id=1, source_target_pairs={{0,1},{1,2},{2,3},{3,4},{4,5},{5,6},{6,7},{7,0},{8,9},{9,10},{10,1... | collective-permute-start | bytes 786440 | tf_op jit(solution)/shard_map/while/body/eval_jaxpr/ppermute | solution.py:13
  159.7 8.6 %collective-permute-start.1 = (bf16[2,128,2,128]{3,1,2,0:T(8,128)(2,1)S(1)}, bf16[2,128,2,128]{3,1,2,0:T(8,128)(2,1)S(1)}, u32[]{:S(2)}, u32[]{:S(2)}) collective-permute-start(bf16[2,128,2,128]{3,1,2,0:T(8,128)(2,1)S(1)} %copy.54), channel_id=1, source_target_pairs={{0,1},{1,2},{2,3},{3,4},{4,5},{5,6},{6,7},{7,0},{8,9},{9,10},{10,1... | collective-permute-start | bytes 393224 | tf_op jit(solution)/shard_map/while/body/eval_jaxpr/ppermute | solution.py:13
  162.0 11.1 %collective-permute-start.2 = (f32[2,128,2,128]{3,1,2,0:T(8,128)}, f32[2,128,2,128]{3,1,2,0:T(8,128)S(1)}, u32[]{:S(2)}, u32[]{:S(2)}) collective-permute-start(f32[2,128,2,128]{3,1,2,0:T(8,128)} %maximum_add_fusion.2), channel_id=1, source_target_pairs={{0,1},{1,2},{2,3},{3,4},{4,5},{5,6},{6,7},{7,0},{8,9},{9,10},{10,1... | collective-permute-start | bytes 786440 | tf_op jit(solution)/shard_map/while/body/eval_jaxpr/ppermute | solution.py:13
  173.1 7.7 %collective-permute-start.1 = (bf16[2,128,2,128]{3,1,2,0:T(8,128)(2,1)S(1)}, bf16[2,128,2,128]{3,1,2,0:T(8,128)(2,1)S(1)}, u32[]{:S(2)}, u32[]{:S(2)}) collective-permute-start(bf16[2,128,2,128]{3,1,2,0:T(8,128)(2,1)S(1)} %copy.54), channel_id=1, source_target_pairs={{0,1},{1,2},{2,3},{3,4},{4,5},{5,6},{6,7},{7,0},{8,9},{9,10},{10,1... | collective-permute-start | bytes 393224 | tf_op jit(solution)/shard_map/while/body/eval_jaxpr/ppermute | solution.py:13
  175.4 9.3 %collective-permute-start.2 = (f32[2,128,2,128]{3,1,2,0:T(8,128)}, f32[2,128,2,128]{3,1,2,0:T(8,128)S(1)}, u32[]{:S(2)}, u32[]{:S(2)}) collective-permute-start(f32[2,128,2,128]{3,1,2,0:T(8,128)} %maximum_add_fusion.2), channel_id=1, source_target_pairs={{0,1},{1,2},{2,3},{3,4},{4,5},{5,6},{6,7},{7,0},{8,9},{9,10},{10,1... | collective-permute-start | bytes 786440 | tf_op jit(solution)/shard_map/while/body/eval_jaxpr/ppermute | solution.py:13
  184.7 0.7 copy-start
Sparse Core Ops, SparseCore 0:
  185.5 31.2 all-reduce.1
where the time goes:
time: 226 us
  waiting for transfers between devices  171 us (76%)
  matrix products  19.9 us (9%)
  between operations  14.2 us (6%)
  local copies, waits for them, and re-layouts  8.24 us (4%)
  other arithmetic  7.6 us (3%)
  starting transfers between devices  3.98 us (2%)
    ppermute x24, waiting for transfers between devices, from_behind(): lax.ppermute(value, axis, [(i, (i + by) % peers) for i in range(peers)])  140 us
    psum x1, waiting for transfers between devices, local(): summed = lax.psum(grads_acc, 'pb')  30.3 us
    add x8, other arithmetic, grad_step(): grads_acc = grads_acc + jnp.stack([dk_part, dv_part])  5.9 us
    dot_general x16, matrix products, block_scores(): jnp.einsum('qhd,khd->hqk', query_blk, key_blk, preferred_element_type=jnp...  5.65 us
    dot_general x16, matrix products, block_scores(): jnp.einsum('qhd,khd->hqk', grad_blk, value_blk, preferred_element_type=jn...  5.56 us
    unnamed x15, local copies, waits for them, and re-layouts  5.08 us
  transfers between devices with their start and end apart: 25, of which 25 were waited for; matrix products, arithmetic and copies ran while one was open for 13% of the time, Pallas kernels for 0%

commit v1 on v0

--- a/solution.py
+++ b/solution.py
@@ -3,9 +3,15 @@
 import jax.numpy as jnp
 from jax import lax
 from jax.sharding import PartitionSpec as P
+from jax.lax import all_gather
 
 H = 2
 DH = 128
+
+
+def treat_lots_all_over_axis(w_in):
+    frame_out = all_gather(w_in, axis_name="pb").sum(axis=0)
+    return frame_out
 
 
 def from_behind(value, axis, by):
@@ -102,7 +108,7 @@
     )
     key_vals, grads_acc, dq_acc = lax.fori_loop(0, cycle_size, grad_step, start)
     dq = dq_acc.reshape(query_rows, H * DH)
-    summed = lax.psum(grads_acc, "pb")
+    summed = treat_lots_all_over_axis(grads_acc)
     return (dq, summed[0].reshape(key_rows, H * DH), summed[1].reshape(key_rows, H * DH))
 
 

time: 226 us -> 211 us (0.934)
  waiting for transfers between devices: 171 us -> 155 us
    psum x1 -> x0, waiting for transfers between devices: 30.3 us -> none  [local(): summed = lax.psum(grads_acc, 'pb')]
    all_gather x0 -> x1, waiting for transfers between devices: none -> 14.8 us  [treat_lots_all_over_axis(): frame_out = all_gather(w_in, axis_name='pb').sum(axis=0)]
    unnamed x15 -> x17, local copies, waits for them, and re-layouts: 5.08 us -> 6.59 us
where the time goes in v1:
time: 211 us
  waiting for transfers between devices  155 us (73%)
  matrix products  19.9 us (9%)
  between operations  14.2 us (7%)
  other arithmetic  8.84 us (4%)
  local copies, waits for them, and re-layouts  8.05 us (4%)
  starting transfers between devices  3.98 us (2%)
    ppermute x24, waiting for transfers between devices, from_behind(): lax.ppermute(value, axis, [(i, (i + by) % peers) for i in range(peers)])  141 us
    all_gather x1, waiting for transfers between devices, treat_lots_all_over_axis(): frame_out = all_gather(w_in, axis_name='pb').sum(axis=0)  14.8 us
    unnamed x17, local copies, waits for them, and re-layouts  6.59 us
    add x8, other arithmetic, grad_step(): grads_acc = grads_acc + jnp.stack([dk_part, dv_part])  5.86 us
    dot_general x16, matrix products, block_scores(): jnp.einsum('qhd,khd->hqk', query_blk, key_blk, preferred_element_type=jnp...  5.64 us
    dot_general x16, matrix products, block_scores(): jnp.einsum('qhd,khd->hqk', grad_blk, value_blk, preferred_element_type=jn...  5.47 us
  transfers between devices with their start and end apart: 25, of which 25 were waited for; matrix products, arithmetic and copies ran while one was open for 13% of the time, Pallas kernels for 0%

profile of v1, /device:TPU:0, one launch (start us, length us, event | category | flops | bytes accessed | tf_op | source)
XLA Modules:
  0.0 211.1 jit_solution(11502665543856636821)
XLA Ops:
  7.2 1.2 copy.38
  8.8 0.8 copy-done.1
  10.0 0.6 copy-done.2
  10.7 0.7 copy-done.3
  11.7 66.0 %while.32 = (s32[]{:T(128)}, bf16[2,128,2,128]{3,1,2,0:T(8,128)(2,1)S(1)}, f32[2,1024]{1,0:T(2,128)S(1)}, f32[2,1024]{1,0:T(2,128)S(1)}, f32[2,1024]{1,0:T(2,128...) while((s32[]{:T(128)}, ...), condition=%wide.region_4.0_spmd.clone, body=%wide.region_0.0_spmd.clone.sunk | while | flops 136067072 | bytes 5259408 | solution.py:90
  11.7 3.0 %collective-permute-start = (bf16[2,128,2,128]{3,1,2,0:T(8,128)(2,1)S(1)}, bf16[2,128,2,128]{3,1,2,0:T(8,128)(2,1)S(1)}, u32[]{:S(2)}, u32[]{:S(2)}) collective-permute-start(bf16[2,128,2,128]{3,1,2,0:T(8,128)(2,1)S(1)} %copy.60), channel_id=1, source_target_pairs={{0,1},{1,2},{2,3},{3,4},{4,5},{5,6},{6,7},{7,0},{8,9},{9,10},{10,1... | collective-permute-start | bytes 393224 | tf_op jit(solution)/shard_map/while/body/eval_jaxpr/ppermute | solution.py:19
  15.7 5.7 %collective-permute-done = bf16[2,128,2,128]{3,1,2,0:T(8,128)(2,1)S(1)} collective-permute-done((bf16[2,128,2,128]{3,1,2,0:T(8,128)(2,1)S(1)}, bf16[2,128,2,128]{3,1,2,0:T(8,128)(2,1)S(1)}, u32[]{:S(2)}, u32[]{:S(2)}) %collective-permute-start) | collective-permute-done | bytes 131104 | tf_op jit(solution)/shard_map/while/body/eval_jaxpr/ppermute | solution.py:19
  22.3 6.8 %collective-permute-done = bf16[2,128,2,128]{3,1,2,0:T(8,128)(2,1)S(1)} collective-permute-done((bf16[2,128,2,128]{3,1,2,0:T(8,128)(2,1)S(1)}, bf16[2,128,2,128]{3,1,2,0:T(8,128)(2,1)S(1)}, u32[]{:S(2)}, u32[]{:S(2)}) %collective-permute-start) | collective-permute-done | bytes 131104 | tf_op jit(solution)/shard_map/while/body/eval_jaxpr/ppermute | solution.py:19
  30.0 6.8 %collective-permute-done = bf16[2,128,2,128]{3,1,2,0:T(8,128)(2,1)S(1)} collective-permute-done((bf16[2,128,2,128]{3,1,2,0:T(8,128)(2,1)S(1)}, bf16[2,128,2,128]{3,1,2,0:T(8,128)(2,1)S(1)}, u32[]{:S(2)}, u32[]{:S(2)}) %collective-permute-start) | collective-permute-done | bytes 131104 | tf_op jit(solution)/shard_map/while/body/eval_jaxpr/ppermute | solution.py:19
  37.7 6.8 %collective-permute-done = bf16[2,128,2,128]{3,1,2,0:T(8,128)(2,1)S(1)} collective-permute-done((bf16[2,128,2,128]{3,1,2,0:T(8,128)(2,1)S(1)}, bf16[2,128,2,128]{3,1,2,0:T(8,128)(2,1)S(1)}, u32[]{:S(2)}, u32[]{:S(2)}) %collective-permute-start) | collective-permute-done | bytes 131104 | tf_op jit(solution)/shard_map/while/body/eval_jaxpr/ppermute | solution.py:19
  45.5 6.8 %collective-permute-done = bf16[2,128,2,128]{3,1,2,0:T(8,128)(2,1)S(1)} collective-permute-done((bf16[2,128,2,128]{3,1,2,0:T(8,128)(2,1)S(1)}, bf16[2,128,2,128]{3,1,2,0:T(8,128)(2,1)S(1)}, u32[]{:S(2)}, u32[]{:S(2)}) %collective-permute-start) | collective-permute-done | bytes 131104 | tf_op jit(solution)/shard_map/while/body/eval_jaxpr/ppermute | solution.py:19
  53.2 7.9 %collective-permute-done = bf16[2,128,2,128]{3,1,2,0:T(8,128)(2,1)S(1)} collective-permute-done((bf16[2,128,2,128]{3,1,2,0:T(8,128)(2,1)S(1)}, bf16[2,128,2,128]{3,1,2,0:T(8,128)(2,1)S(1)}, u32[]{:S(2)}, u32[]{:S(2)}) %collective-permute-start) | collective-permute-done | bytes 131104 | tf_op jit(solution)/shard_map/while/body/eval_jaxpr/ppermute | solution.py:19
  62.1 7.3 %collective-permute-done = bf16[2,128,2,128]{3,1,2,0:T(8,128)(2,1)S(1)} collective-permute-done((bf16[2,128,2,128]{3,1,2,0:T(8,128)(2,1)S(1)}, bf16[2,128,2,128]{3,1,2,0:T(8,128)(2,1)S(1)}, u32[]{:S(2)}, u32[]{:S(2)}) %collective-permute-start) | collective-permute-done | bytes 131104 | tf_op jit(solution)/shard_map/while/body/eval_jaxpr/ppermute | solution.py:19
  70.3 7.4 %collective-permute-done = bf16[2,128,2,128]{3,1,2,0:T(8,128)(2,1)S(1)} collective-permute-done((bf16[2,128,2,128]{3,1,2,0:T(8,128)(2,1)S(1)}, bf16[2,128,2,128]{3,1,2,0:T(8,128)(2,1)S(1)}, u32[]{:S(2)}, u32[]{:S(2)}) %collective-permute-start) | collective-permute-done | bytes 131104 | tf_op jit(solution)/shard_map/while/body/eval_jaxpr/ppermute | solution.py:19
  77.8 106.8 %while.33 = (s32[]{:T(128)}, bf16[2,128,2,128]{3,1,2,0:T(8,128)(2,1)S(1)}, f32[2,128,2,128]{3,1,2,0:T(8,128)S(1)}, f32[1024,2,128]{2,0,1:T(8,128)S(1)}, bf16[102...) while((s32[]{:T(128)}, ...), condition=%wide.region_6.0_spmd.clone, body=%wide.region_5.0_spmd.clone.sunk | while | flops 338067456 | bytes 12009663 | solution.py:109
  79.4 0.7 maximum_add_fusion.2
  80.1 0.4 fusion.78
  80.5 5.5 %collective-permute-done.1 = bf16[2,128,2,128]{3,1,2,0:T(8,128)(2,1)S(1)} collective-permute-done((bf16[2,128,2,128]{3,1,2,0:T(8,128)(2,1)S(1)}, bf16[2,128,2,128]{3,1,2,0:T(8,128)(2,1)S(1)}, u32[]{:S(2)}, u32[]{:S(2)}) %collective-permute-start.1) | collective-permute-done | bytes 131104 | tf_op jit(solution)/shard_map/while/body/eval_jaxpr/ppermute | solution.py:19
  86.0 6.0 %collective-permute-done.2 = f32[2,128,2,128]{3,1,2,0:T(8,128)S(1)} collective-permute-done((f32[2,128,2,128]{3,1,2,0:T(8,128)}, f32[2,128,2,128]{3,1,2,0:T(8,128)S(1)}, u32[]{:S(2)}, u32[]{:S(2)}) %collective-permute-start.2) | collective-permute-done | bytes 262176 | tf_op jit(solution)/shard_map/while/body/eval_jaxpr/ppermute | solution.py:19
  93.5 0.7 maximum_add_fusion.2
  94.3 0.4 fusion.78
  94.7 6.2 %collective-permute-done.1 = bf16[2,128,2,128]{3,1,2,0:T(8,128)(2,1)S(1)} collective-permute-done((bf16[2,128,2,128]{3,1,2,0:T(8,128)(2,1)S(1)}, bf16[2,128,2,128]{3,1,2,0:T(8,128)(2,1)S(1)}, u32[]{:S(2)}, u32[]{:S(2)}) %collective-permute-start.1) | collective-permute-done | bytes 131104 | tf_op jit(solution)/shard_map/while/body/eval_jaxpr/ppermute | solution.py:19
  100.9 5.2 %collective-permute-done.2 = f32[2,128,2,128]{3,1,2,0:T(8,128)S(1)} collective-permute-done((f32[2,128,2,128]{3,1,2,0:T(8,128)}, f32[2,128,2,128]{3,1,2,0:T(8,128)S(1)}, u32[]{:S(2)}, u32[]{:S(2)}) %collective-permute-start.2) | collective-permute-done | bytes 262176 | tf_op jit(solution)/shard_map/while/body/eval_jaxpr/ppermute | solution.py:19
  107.7 0.7 maximum_add_fusion.2
  108.9 5.6 %collective-permute-done.1 = bf16[2,128,2,128]{3,1,2,0:T(8,128)(2,1)S(1)} collective-permute-done((bf16[2,128,2,128]{3,1,2,0:T(8,128)(2,1)S(1)}, bf16[2,128,2,128]{3,1,2,0:T(8,128)(2,1)S(1)}, u32[]{:S(2)}, u32[]{:S(2)}) %collective-permute-start.1) | collective-permute-done | bytes 131104 | tf_op jit(solution)/shard_map/while/body/eval_jaxpr/ppermute | solution.py:19
  114.5 5.2 %collective-permute-done.2 = f32[2,128,2,128]{3,1,2,0:T(8,128)S(1)} collective-permute-done((f32[2,128,2,128]{3,1,2,0:T(8,128)}, f32[2,128,2,128]{3,1,2,0:T(8,128)S(1)}, u32[]{:S(2)}, u32[]{:S(2)}) %collective-permute-start.2) | collective-permute-done | bytes 262176 | tf_op jit(solution)/shard_map/while/body/eval_jaxpr/ppermute | solution.py:19
  121.2 0.7 maximum_add_fusion.2
  122.4 5.7 %collective-permute-done.1 = bf16[2,128,2,128]{3,1,2,0:T(8,128)(2,1)S(1)} collective-permute-done((bf16[2,128,2,128]{3,1,2,0:T(8,128)(2,1)S(1)}, bf16[2,128,2,128]{3,1,2,0:T(8,128)(2,1)S(1)}, u32[]{:S(2)}, u32[]{:S(2)}) %collective-permute-start.1) | collective-permute-done | bytes 131104 | tf_op jit(solution)/shard_map/while/body/eval_jaxpr/ppermute | solution.py:19
  128.1 4.9 %collective-permute-done.2 = f32[2,128,2,128]{3,1,2,0:T(8,128)S(1)} collective-permute-done((f32[2,128,2,128]{3,1,2,0:T(8,128)}, f32[2,128,2,128]{3,1,2,0:T(8,128)S(1)}, u32[]{:S(2)}, u32[]{:S(2)}) %collective-permute-start.2) | collective-permute-done | bytes 262176 | tf_op jit(solution)/shard_map/while/body/eval_jaxpr/ppermute | solution.py:19
  134.6 0.7 maximum_add_fusion.2
  135.7 5.9 %collective-permute-done.1 = bf16[2,128,2,128]{3,1,2,0:T(8,128)(2,1)S(1)} collective-permute-done((bf16[2,128,2,128]{3,1,2,0:T(8,128)(2,1)S(1)}, bf16[2,128,2,128]{3,1,2,0:T(8,128)(2,1)S(1)}, u32[]{:S(2)}, u32[]{:S(2)}) %collective-permute-start.1) | collective-permute-done | bytes 131104 | tf_op jit(solution)/shard_map/while/body/eval_jaxpr/ppermute | solution.py:19
  141.6 4.8 %collective-permute-done.2 = f32[2,128,2,128]{3,1,2,0:T(8,128)S(1)} collective-permute-done((f32[2,128,2,128]{3,1,2,0:T(8,128)}, f32[2,128,2,128]{3,1,2,0:T(8,128)S(1)}, u32[]{:S(2)}, u32[]{:S(2)}) %collective-permute-start.2) | collective-permute-done | bytes 262176 | tf_op jit(solution)/shard_map/while/body/eval_jaxpr/ppermute | solution.py:19
  147.9 0.7 maximum_add_fusion.2
  149.1 5.9 %collective-permute-done.1 = bf16[2,128,2,128]{3,1,2,0:T(8,128)(2,1)S(1)} collective-permute-done((bf16[2,128,2,128]{3,1,2,0:T(8,128)(2,1)S(1)}, bf16[2,128,2,128]{3,1,2,0:T(8,128)(2,1)S(1)}, u32[]{:S(2)}, u32[]{:S(2)}) %collective-permute-start.1) | collective-permute-done | bytes 131104 | tf_op jit(solution)/shard_map/while/body/eval_jaxpr/ppermute | solution.py:19
  155.0 4.8 %collective-permute-done.2 = f32[2,128,2,128]{3,1,2,0:T(8,128)S(1)} collective-permute-done((f32[2,128,2,128]{3,1,2,0:T(8,128)}, f32[2,128,2,128]{3,1,2,0:T(8,128)S(1)}, u32[]{:S(2)}, u32[]{:S(2)}) %collective-permute-start.2) | collective-permute-done | bytes 262176 | tf_op jit(solution)/shard_map/while/body/eval_jaxpr/ppermute | solution.py:19
  161.3 0.7 maximum_add_fusion.2
  162.0 0.4 fusion.78
  162.4 5.9 %collective-permute-done.1 = bf16[2,128,2,128]{3,1,2,0:T(8,128)(2,1)S(1)} collective-permute-done((bf16[2,128,2,128]{3,1,2,0:T(8,128)(2,1)S(1)}, bf16[2,128,2,128]{3,1,2,0:T(8,128)(2,1)S(1)}, u32[]{:S(2)}, u32[]{:S(2)}) %collective-permute-start.1) | collective-permute-done | bytes 131104 | tf_op jit(solution)/shard_map/while/body/eval_jaxpr/ppermute | solution.py:19
  168.3 4.8 %collective-permute-done.2 = f32[2,128,2,128]{3,1,2,0:T(8,128)S(1)} collective-permute-done((f32[2,128,2,128]{3,1,2,0:T(8,128)}, f32[2,128,2,128]{3,1,2,0:T(8,128)S(1)}, u32[]{:S(2)}, u32[]{:S(2)}) %collective-permute-start.2) | collective-permute-done | bytes 262176 | tf_op jit(solution)/shard_map/while/body/eval_jaxpr/ppermute | solution.py:19
  174.6 0.7 maximum_add_fusion.2
  175.8 5.0 %collective-permute-done.1 = bf16[2,128,2,128]{3,1,2,0:T(8,128)(2,1)S(1)} collective-permute-done((bf16[2,128,2,128]{3,1,2,0:T(8,128)(2,1)S(1)}, bf16[2,128,2,128]{3,1,2,0:T(8,128)(2,1)S(1)}, u32[]{:S(2)}, u32[]{:S(2)}) %collective-permute-start.1) | collective-permute-done | bytes 131104 | tf_op jit(solution)/shard_map/while/body/eval_jaxpr/ppermute | solution.py:19
  180.8 3.8 %collective-permute-done.2 = f32[2,128,2,128]{3,1,2,0:T(8,128)S(1)} collective-permute-done((f32[2,128,2,128]{3,1,2,0:T(8,128)}, f32[2,128,2,128]{3,1,2,0:T(8,128)S(1)}, u32[]{:S(2)}, u32[]{:S(2)}) %collective-permute-start.2) | collective-permute-done | bytes 262176 | tf_op jit(solution)/shard_map/while/body/eval_jaxpr/ppermute | solution.py:19
  184.6 0.7 copy-done
  185.4 1.1 copy_bitcast_fusion
  186.4 14.8 %all-gather.3.cloned.1.call-done = f32[8,128,2,128]{3,1,2,0:T(8,128)} async-done(((f32[2,128,2,128]{3,1,2,0:T(8,128)}), f32[8,128,2,128]{3,1,2,0:T(8,128)}) %all-gather.3.cloned.1.call-update) | async-done | bytes 1048592 | tf_op jit(solution)/shard_map/all_gather | solution.py:13
  201.2 1.3 reduce_sum.27
  202.6 0.8 copy.48
  203.5 0.8 copy.49
  (146 shorter events, 22.8 us)
Async XLA Ops:
  7.2 194.0 %all-gather.3.cloned.1.call-start = ((), (), s32[]{:S(2)}) async-start(), calls=%async_computation | async-start | bytes 1310720 | tf_op jit(solution)/shard_map/all_gather | solution.py:13
  8.5 1.0 copy-start.1
  9.8 0.8 copy-start.2
  10.6 0.8 copy-start.3
  11.7 9.6 %collective-permute-start = (bf16[2,128,2,128]{3,1,2,0:T(8,128)(2,1)S(1)}, bf16[2,128,2,128]{3,1,2,0:T(8,128)(2,1)S(1)}, u32[]{:S(2)}, u32[]{:S(2)}) collective-permute-start(bf16[2,128,2,128]{3,1,2,0:T(8,128)(2,1)S(1)} %copy.60), channel_id=1, source_target_pairs={{0,1},{1,2},{2,3},{3,4},{4,5},{5,6},{6,7},{7,0},{8,9},{9,10},{10,1... | collective-permute-start | bytes 393224 | tf_op jit(solution)/shard_map/while/body/eval_jaxpr/ppermute | solution.py:19
  21.3 7.7 %collective-permute-start = (bf16[2,128,2,128]{3,1,2,0:T(8,128)(2,1)S(1)}, bf16[2,128,2,128]{3,1,2,0:T(8,128)(2,1)S(1)}, u32[]{:S(2)}, u32[]{:S(2)}) collective-permute-start(bf16[2,128,2,128]{3,1,2,0:T(8,128)(2,1)S(1)} %copy.60), channel_id=1, source_target_pairs={{0,1},{1,2},{2,3},{3,4},{4,5},{5,6},{6,7},{7,0},{8,9},{9,10},{10,1... | collective-permute-start | bytes 393224 | tf_op jit(solution)/shard_map/while/body/eval_jaxpr/ppermute | solution.py:19
  29.1 7.7 %collective-permute-start = (bf16[2,128,2,128]{3,1,2,0:T(8,128)(2,1)S(1)}, bf16[2,128,2,128]{3,1,2,0:T(8,128)(2,1)S(1)}, u32[]{:S(2)}, u32[]{:S(2)}) collective-permute-start(bf16[2,128,2,128]{3,1,2,0:T(8,128)(2,1)S(1)} %copy.60), channel_id=1, source_target_pairs={{0,1},{1,2},{2,3},{3,4},{4,5},{5,6},{6,7},{7,0},{8,9},{9,10},{10,1... | collective-permute-start | bytes 393224 | tf_op jit(solution)/shard_map/while/body/eval_jaxpr/ppermute | solution.py:19
  36.8 7.7 %collective-permute-start = (bf16[2,128,2,128]{3,1,2,0:T(8,128)(2,1)S(1)}, bf16[2,128,2,128]{3,1,2,0:T(8,128)(2,1)S(1)}, u32[]{:S(2)}, u32[]{:S(2)}) collective-permute-start(bf16[2,128,2,128]{3,1,2,0:T(8,128)(2,1)S(1)} %copy.60), channel_id=1, source_target_pairs={{0,1},{1,2},{2,3},{3,4},{4,5},{5,6},{6,7},{7,0},{8,9},{9,10},{10,1... | collective-permute-start | bytes 393224 | tf_op jit(solution)/shard_map/while/body/eval_jaxpr/ppermute | solution.py:19
  44.5 7.7 %collective-permute-start = (bf16[2,128,2,128]{3,1,2,0:T(8,128)(2,1)S(1)}, bf16[2,128,2,128]{3,1,2,0:T(8,128)(2,1)S(1)}, u32[]{:S(2)}, u32[]{:S(2)}) collective-permute-start(bf16[2,128,2,128]{3,1,2,0:T(8,128)(2,1)S(1)} %copy.60), channel_id=1, source_target_pairs={{0,1},{1,2},{2,3},{3,4},{4,5},{5,6},{6,7},{7,0},{8,9},{9,10},{10,1... | collective-permute-start | bytes 393224 | tf_op jit(solution)/shard_map/while/body/eval_jaxpr/ppermute | solution.py:19
  52.3 8.8 %collective-permute-start = (bf16[2,128,2,128]{3,1,2,0:T(8,128)(2,1)S(1)}, bf16[2,128,2,128]{3,1,2,0:T(8,128)(2,1)S(1)}, u32[]{:S(2)}, u32[]{:S(2)}) collective-permute-start(bf16[2,128,2,128]{3,1,2,0:T(8,128)(2,1)S(1)} %copy.60), channel_id=1, source_target_pairs={{0,1},{1,2},{2,3},{3,4},{4,5},{5,6},{6,7},{7,0},{8,9},{9,10},{10,1... | collective-permute-start | bytes 393224 | tf_op jit(solution)/shard_map/while/body/eval_jaxpr/ppermute | solution.py:19
  61.1 8.3 %collective-permute-start = (bf16[2,128,2,128]{3,1,2,0:T(8,128)(2,1)S(1)}, bf16[2,128,2,128]{3,1,2,0:T(8,128)(2,1)S(1)}, u32[]{:S(2)}, u32[]{:S(2)}) collective-permute-start(bf16[2,128,2,128]{3,1,2,0:T(8,128)(2,1)S(1)} %copy.60), channel_id=1, source_target_pairs={{0,1},{1,2},{2,3},{3,4},{4,5},{5,6},{6,7},{7,0},{8,9},{9,10},{10,1... | collective-permute-start | bytes 393224 | tf_op jit(solution)/shard_map/while/body/eval_jaxpr/ppermute | solution.py:19
  69.4 8.3 %collective-permute-start = (bf16[2,128,2,128]{3,1,2,0:T(8,128)(2,1)S(1)}, bf16[2,128,2,128]{3,1,2,0:T(8,128)(2,1)S(1)}, u32[]{:S(2)}, u32[]{:S(2)}) collective-permute-start(bf16[2,128,2,128]{3,1,2,0:T(8,128)(2,1)S(1)} %copy.60), channel_id=1, source_target_pairs={{0,1},{1,2},{2,3},{3,4},{4,5},{5,6},{6,7},{7,0},{8,9},{9,10},{10,1... | collective-permute-start | bytes 393224 | tf_op jit(solution)/shard_map/while/body/eval_jaxpr/ppermute | solution.py:19
  77.8 8.2 %collective-permute-start.1 = (bf16[2,128,2,128]{3,1,2,0:T(8,128)(2,1)S(1)}, bf16[2,128,2,128]{3,1,2,0:T(8,128)(2,1)S(1)}, u32[]{:S(2)}, u32[]{:S(2)}) collective-permute-start(bf16[2,128,2,128]{3,1,2,0:T(8,128)(2,1)S(1)} %copy.74), channel_id=1, source_target_pairs={{0,1},{1,2},{2,3},{3,4},{4,5},{5,6},{6,7},{7,0},{8,9},{9,10},{10,1... | collective-permute-start | bytes 393224 | tf_op jit(solution)/shard_map/while/body/eval_jaxpr/ppermute | solution.py:19
  80.1 11.9 %collective-permute-start.2 = (f32[2,128,2,128]{3,1,2,0:T(8,128)}, f32[2,128,2,128]{3,1,2,0:T(8,128)S(1)}, u32[]{:S(2)}, u32[]{:S(2)}) collective-permute-start(f32[2,128,2,128]{3,1,2,0:T(8,128)} %maximum_add_fusion.2), channel_id=1, source_target_pairs={{0,1},{1,2},{2,3},{3,4},{4,5},{5,6},{6,7},{7,0},{8,9},{9,10},{10,1... | collective-permute-start | bytes 786440 | tf_op jit(solution)/shard_map/while/body/eval_jaxpr/ppermute | solution.py:19
  92.0 8.9 %collective-permute-start.1 = (bf16[2,128,2,128]{3,1,2,0:T(8,128)(2,1)S(1)}, bf16[2,128,2,128]{3,1,2,0:T(8,128)(2,1)S(1)}, u32[]{:S(2)}, u32[]{:S(2)}) collective-permute-start(bf16[2,128,2,128]{3,1,2,0:T(8,128)(2,1)S(1)} %copy.74), channel_id=1, source_target_pairs={{0,1},{1,2},{2,3},{3,4},{4,5},{5,6},{6,7},{7,0},{8,9},{9,10},{10,1... | collective-permute-start | bytes 393224 | tf_op jit(solution)/shard_map/while/body/eval_jaxpr/ppermute | solution.py:19
  94.3 11.9 %collective-permute-start.2 = (f32[2,128,2,128]{3,1,2,0:T(8,128)}, f32[2,128,2,128]{3,1,2,0:T(8,128)S(1)}, u32[]{:S(2)}, u32[]{:S(2)}) collective-permute-start(f32[2,128,2,128]{3,1,2,0:T(8,128)} %maximum_add_fusion.2), channel_id=1, source_target_pairs={{0,1},{1,2},{2,3},{3,4},{4,5},{5,6},{6,7},{7,0},{8,9},{9,10},{10,1... | collective-permute-start | bytes 786440 | tf_op jit(solution)/shard_map/while/body/eval_jaxpr/ppermute | solution.py:19
  106.2 8.3 %collective-permute-start.1 = (bf16[2,128,2,128]{3,1,2,0:T(8,128)(2,1)S(1)}, bf16[2,128,2,128]{3,1,2,0:T(8,128)(2,1)S(1)}, u32[]{:S(2)}, u32[]{:S(2)}) collective-permute-start(bf16[2,128,2,128]{3,1,2,0:T(8,128)(2,1)S(1)} %copy.74), channel_id=1, source_target_pairs={{0,1},{1,2},{2,3},{3,4},{4,5},{5,6},{6,7},{7,0},{8,9},{9,10},{10,1... | collective-permute-start | bytes 393224 | tf_op jit(solution)/shard_map/while/body/eval_jaxpr/ppermute | solution.py:19
  108.4 11.2 %collective-permute-start.2 = (f32[2,128,2,128]{3,1,2,0:T(8,128)}, f32[2,128,2,128]{3,1,2,0:T(8,128)S(1)}, u32[]{:S(2)}, u32[]{:S(2)}) collective-permute-start(f32[2,128,2,128]{3,1,2,0:T(8,128)} %maximum_add_fusion.2), channel_id=1, source_target_pairs={{0,1},{1,2},{2,3},{3,4},{4,5},{5,6},{6,7},{7,0},{8,9},{9,10},{10,1... | collective-permute-start | bytes 786440 | tf_op jit(solution)/shard_map/while/body/eval_jaxpr/ppermute | solution.py:19
  119.7 8.4 %collective-permute-start.1 = (bf16[2,128,2,128]{3,1,2,0:T(8,128)(2,1)S(1)}, bf16[2,128,2,128]{3,1,2,0:T(8,128)(2,1)S(1)}, u32[]{:S(2)}, u32[]{:S(2)}) collective-permute-start(bf16[2,128,2,128]{3,1,2,0:T(8,128)(2,1)S(1)} %copy.74), channel_id=1, source_target_pairs={{0,1},{1,2},{2,3},{3,4},{4,5},{5,6},{6,7},{7,0},{8,9},{9,10},{10,1... | collective-permute-start | bytes 393224 | tf_op jit(solution)/shard_map/while/body/eval_jaxpr/ppermute | solution.py:19
  122.0 11.1 %collective-permute-start.2 = (f32[2,128,2,128]{3,1,2,0:T(8,128)}, f32[2,128,2,128]{3,1,2,0:T(8,128)S(1)}, u32[]{:S(2)}, u32[]{:S(2)}) collective-permute-start(f32[2,128,2,128]{3,1,2,0:T(8,128)} %maximum_add_fusion.2), channel_id=1, source_target_pairs={{0,1},{1,2},{2,3},{3,4},{4,5},{5,6},{6,7},{7,0},{8,9},{9,10},{10,1... | collective-permute-start | bytes 786440 | tf_op jit(solution)/shard_map/while/body/eval_jaxpr/ppermute | solution.py:19
  133.0 8.6 %collective-permute-start.1 = (bf16[2,128,2,128]{3,1,2,0:T(8,128)(2,1)S(1)}, bf16[2,128,2,128]{3,1,2,0:T(8,128)(2,1)S(1)}, u32[]{:S(2)}, u32[]{:S(2)}) collective-permute-start(bf16[2,128,2,128]{3,1,2,0:T(8,128)(2,1)S(1)} %copy.74), channel_id=1, source_target_pairs={{0,1},{1,2},{2,3},{3,4},{4,5},{5,6},{6,7},{7,0},{8,9},{9,10},{10,1... | collective-permute-start | bytes 393224 | tf_op jit(solution)/shard_map/while/body/eval_jaxpr/ppermute | solution.py:19
  135.3 11.1 %collective-permute-start.2 = (f32[2,128,2,128]{3,1,2,0:T(8,128)}, f32[2,128,2,128]{3,1,2,0:T(8,128)S(1)}, u32[]{:S(2)}, u32[]{:S(2)}) collective-permute-start(f32[2,128,2,128]{3,1,2,0:T(8,128)} %maximum_add_fusion.2), channel_id=1, source_target_pairs={{0,1},{1,2},{2,3},{3,4},{4,5},{5,6},{6,7},{7,0},{8,9},{9,10},{10,1... | collective-permute-start | bytes 786440 | tf_op jit(solution)/shard_map/while/body/eval_jaxpr/ppermute | solution.py:19
  146.4 8.6 %collective-permute-start.1 = (bf16[2,128,2,128]{3,1,2,0:T(8,128)(2,1)S(1)}, bf16[2,128,2,128]{3,1,2,0:T(8,128)(2,1)S(1)}, u32[]{:S(2)}, u32[]{:S(2)}) collective-permute-start(bf16[2,128,2,128]{3,1,2,0:T(8,128)(2,1)S(1)} %copy.74), channel_id=1, source_target_pairs={{0,1},{1,2},{2,3},{3,4},{4,5},{5,6},{6,7},{7,0},{8,9},{9,10},{10,1... | collective-permute-start | bytes 393224 | tf_op jit(solution)/shard_map/while/body/eval_jaxpr/ppermute | solution.py:19
  148.7 11.1 %collective-permute-start.2 = (f32[2,128,2,128]{3,1,2,0:T(8,128)}, f32[2,128,2,128]{3,1,2,0:T(8,128)S(1)}, u32[]{:S(2)}, u32[]{:S(2)}) collective-permute-start(f32[2,128,2,128]{3,1,2,0:T(8,128)} %maximum_add_fusion.2), channel_id=1, source_target_pairs={{0,1},{1,2},{2,3},{3,4},{4,5},{5,6},{6,7},{7,0},{8,9},{9,10},{10,1... | collective-permute-start | bytes 786440 | tf_op jit(solution)/shard_map/while/body/eval_jaxpr/ppermute | solution.py:19
  159.7 8.6 %collective-permute-start.1 = (bf16[2,128,2,128]{3,1,2,0:T(8,128)(2,1)S(1)}, bf16[2,128,2,128]{3,1,2,0:T(8,128)(2,1)S(1)}, u32[]{:S(2)}, u32[]{:S(2)}) collective-permute-start(bf16[2,128,2,128]{3,1,2,0:T(8,128)(2,1)S(1)} %copy.74), channel_id=1, source_target_pairs={{0,1},{1,2},{2,3},{3,4},{4,5},{5,6},{6,7},{7,0},{8,9},{9,10},{10,1... | collective-permute-start | bytes 393224 | tf_op jit(solution)/shard_map/while/body/eval_jaxpr/ppermute | solution.py:19
  162.0 11.1 %collective-permute-start.2 = (f32[2,128,2,128]{3,1,2,0:T(8,128)}, f32[2,128,2,128]{3,1,2,0:T(8,128)S(1)}, u32[]{:S(2)}, u32[]{:S(2)}) collective-permute-start(f32[2,128,2,128]{3,1,2,0:T(8,128)} %maximum_add_fusion.2), channel_id=1, source_target_pairs={{0,1},{1,2},{2,3},{3,4},{4,5},{5,6},{6,7},{7,0},{8,9},{9,10},{10,1... | collective-permute-start | bytes 786440 | tf_op jit(solution)/shard_map/while/body/eval_jaxpr/ppermute | solution.py:19
  173.1 7.7 %collective-permute-start.1 = (bf16[2,128,2,128]{3,1,2,0:T(8,128)(2,1)S(1)}, bf16[2,128,2,128]{3,1,2,0:T(8,128)(2,1)S(1)}, u32[]{:S(2)}, u32[]{:S(2)}) collective-permute-start(bf16[2,128,2,128]{3,1,2,0:T(8,128)(2,1)S(1)} %copy.74), channel_id=1, source_target_pairs={{0,1},{1,2},{2,3},{3,4},{4,5},{5,6},{6,7},{7,0},{8,9},{9,10},{10,1... | collective-permute-start | bytes 393224 | tf_op jit(solution)/shard_map/while/body/eval_jaxpr/ppermute | solution.py:19
  175.4 9.3 %collective-permute-start.2 = (f32[2,128,2,128]{3,1,2,0:T(8,128)}, f32[2,128,2,128]{3,1,2,0:T(8,128)S(1)}, u32[]{:S(2)}, u32[]{:S(2)}) collective-permute-start(f32[2,128,2,128]{3,1,2,0:T(8,128)} %maximum_add_fusion.2), channel_id=1, source_target_pairs={{0,1},{1,2},{2,3},{3,4},{4,5},{5,6},{6,7},{7,0},{8,9},{9,10},{10,1... | collective-permute-start | bytes 786440 | tf_op jit(solution)/shard_map/while/body/eval_jaxpr/ppermute | solution.py:19
  184.6 0.7 copy-start
Sparse Core Ops, SparseCore 0:
  185.5 15.6 all-gather.2
